TPU v7x, 128 devices: a whole 4x4x4 slice. The times are simulated.
128 devices in a mesh: row: 8 (over y_hi, z), col: 16 (over x, y_lo, core).
Axes of the slice: x: 4, y: 4 (y_hi: 2, y_lo: 2; y = y_hi * 2 + y_lo), z: 4, core: 2. Of those that a mesh axis runs over, the one named last changes fastest.
Arguments:
- obj: float32 [2, 3072, 6144], P(None, 'row', 'col'), may hold values from -6 to 6
- probe: float32 [4, 2, 128, 128], replicated, may hold values from -3 to 3
- positions: int32 [8, 16, 8, 2], P('row', 'col'), may hold values from 0 to 383
- counts: int32 [8, 16], P('row', 'col'), may hold values from 2 to 8, as said below
- offsets: int32 [8, 4], replicated, may hold values from 0 to 3, each once within a row
- measured: float32 [8, 16, 8, 128, 128], P('row', 'col'), may hold values from 0.3 to 5
Outputs:
- new_object: float32 [2, 3072, 6144], P(None, 'row', 'col')
Inputs may be any that keep to these rules, and one draw needn't show every extreme that they name: `counts`: some device uses all 8 slots. At each scan slot the beams have different offsets.
All inputs are finite; a program needn't handle non-finite values.
Results may differ from a plain program's by a relative error of at most 0.0003.
Values sent between devices are 32-bit elements; how exact they have to be, the bound alone decides.
A program may use at most 128 MiB of HBM per device.

v0:
```python
import math

import jax
import jax.numpy as jnp
from jax import lax
from jax.sharding import PartitionSpec as P

P_SIZE = 128
BEAMS = 4
SCANS = 8


EPSILON = 0.5
DAMPING = 0.5


def extended(block, sides, width):
    for axis, dim in sides:
        count = lax.axis_size(axis)
        forward = [(i, i + 1) for i in range(count - 1)]
        backward = [(target, source) for source, target in forward]
        low = lax.ppermute(
            lax.slice_in_dim(block, block.shape[dim] - width, None, axis=dim), axis, forward
        )
        high = lax.ppermute(lax.slice_in_dim(block, 0, width, axis=dim), axis, backward)
        block = jnp.concatenate([low, block, high], axis=dim)
    return block


def shifted(x, axis, by):
    peers = lax.axis_size(axis)
    return lax.ppermute(x, axis, [(i, (i + by) % peers) for i in range(peers)])


def dft_tables(length):
    index = jnp.arange(length, dtype=jnp.int32)
    product = index[:, None] * index[None, :] % length
    angle = product.astype(jnp.float32) * (2.0 * math.pi / length)
    factor_norm = 1.0 / math.sqrt(length)
    return (jnp.cos(angle) * factor_norm, -jnp.sin(angle) * factor_norm)


def transform(real_part, imag_part, table_re, table_im):
    highest = lax.Precision.HIGHEST
    left_re = jnp.einsum("jk,abkl->abjl", table_re, real_part, precision=highest) - jnp.einsum(
        "jk,abkl->abjl", table_im, imag_part, precision=highest
    )
    left_im = jnp.einsum("jk,abkl->abjl", table_re, imag_part, precision=highest) + jnp.einsum(
        "jk,abkl->abjl", table_im, real_part, precision=highest
    )
    out_re = jnp.einsum("abjk,kl->abjl", left_re, table_re, precision=highest) - jnp.einsum(
        "abjk,kl->abjl", left_im, table_im, precision=highest
    )
    out_im = jnp.einsum("abjk,kl->abjl", left_re, table_im, precision=highest) + jnp.einsum(
        "abjk,kl->abjl", left_im, table_re, precision=highest
    )
    return (out_re, out_im)


def on_device(obj, probe, positions, counts, offsets, measured):
    half = P_SIZE // 2
    tile = obj.shape[1]
    framed = extended(obj, (("row", 1), ("col", 2)), half)
    frames = [framed]
    current = framed
    for step in range(3):
        current = shifted(current, "row", -1)
        frames.append(current)
    stacked = jnp.stack(frames)
    spots = positions[0, 0]
    live = (jnp.arange(SCANS) < counts[0, 0]).astype(jnp.float32)
    zero_index = jnp.zeros((), jnp.int32)

    def cut_one(row_at, col_at, which):
        return lax.dynamic_slice(
            stacked, (which, zero_index, row_at, col_at), (1, 2, P_SIZE, P_SIZE)
        )[0]

    def cut_beams(row_at, col_at, slot_offsets):
        return jax.vmap(lambda which: cut_one(row_at, col_at, which))(slot_offsets)

    patches = jax.vmap(cut_beams)(spots[:, 0], spots[:, 1], offsets)
    patch_re = patches[:, :, 0]
    patch_im = patches[:, :, 1]
    probe_re = probe[:, 0][None]
    probe_im = probe[:, 1][None]
    exit_re = probe_re * patch_re - probe_im * patch_im
    exit_im = probe_re * patch_im + probe_im * patch_re
    table_re, table_im = dft_tables(P_SIZE)
    far_re, far_im = transform(exit_re, exit_im, table_re, table_im)
    intensity = jnp.sum(far_re * far_re + far_im * far_im, axis=1)
    factor = measured[0, 0] / jnp.sqrt(intensity + EPSILON)
    back_re, back_im = transform(
        far_re * factor[:, None], far_im * factor[:, None], table_re, -table_im
    )
    live_mask = live[:, None, None, None]
    change_re = (back_re - exit_re) * live_mask
    change_im = (back_im - exit_im) * live_mask
    grad_re = probe_re * change_re + probe_im * change_im
    grad_im = probe_re * change_im - probe_im * change_re
    illum = (probe_re * probe_re + probe_im * probe_im) * live_mask
    contrib = jnp.stack([grad_re, grad_im, illum], axis=2)
    channels = contrib.shape[2]
    side = tile + 2 * half
    accum = jnp.zeros((4, channels, side, side), jnp.float32)

    def add_scan(slot, accum):
        for beam in range(BEAMS):
            start = (offsets[slot, beam], zero_index, spots[slot, 0], spots[slot, 1])
            current = lax.dynamic_slice(accum, start, (1, channels, P_SIZE, P_SIZE))
            accum = lax.dynamic_update_slice(accum, current + contrib[slot, beam][None], start)
        return accum

    accum = lax.fori_loop(0, SCANS, add_scan, accum)
    total = accum[3]
    for step in (2, 1, 0):
        total = shifted(total, "row", 1) + accum[step]
    outer = extended(total, (("row", 1), ("col", 2)), half)
    pieces = ((0, half, 0), (2 * half, tile, 0), (tile + 3 * half, half, tile - half))
    interior = jnp.zeros((channels, tile, tile), jnp.float32)
    for row_src, row_len, row_dst in pieces:
        for col_src, col_len, col_dst in pieces:
            interior = interior.at[:, row_dst : row_dst + row_len, col_dst : col_dst + col_len].add(
                outer[:, row_src : row_src + row_len, col_src : col_src + col_len]
            )
    weight_map = interior[2]
    return obj + interior[:2] / (weight_map + DAMPING)


def solution(mesh):
    return jax.shard_map(
        on_device,
        mesh=mesh,
        in_specs=(
            P(None, "row", "col"),
            P(),
            P("row", "col", None, None),
            P("row", "col"),
            P(),
            P("row", "col", None, None, None),
        ),
        out_specs=P(None, "row", "col"),
        check_vma=False,
    )
```

profile of v0, /device:TPU:105, one launch (start us, length us, event | category | flops | bytes accessed | tf_op | source)
XLA Modules:
  0.0 972.3 jit_solution(10436874361974232276)
XLA Ops:
  10.1 4.5 collective-permute-done.1
  14.9 5.6 collective-permute-start.2
  22.6 4.1 collective-permute-done.2
  26.6 5.5 collective-permute-done.3
  32.9 48.4 %collective-permute-done.4 = f32[2,512,512]{2,1,0:T(8,128)S(1)} collective-permute-done((f32[2,512,512]{2,1,0:T(8,128)S(1)}, f32[2,512,512]{2,1,0:T(8,128)S(1)}, u32[]{:S(2)}, u32[]{:S(2)}) %collective-permute-start.4) | collective-permute-done | bytes 2097184 | tf_op jit(solution)/shard_map/ppermute | solution.py:32
  82.7 49.7 %collective-permute-done.5 = f32[2,512,512]{2,1,0:T(8,128)} collective-permute-done((f32[2,512,512]{2,1,0:T(8,128)S(1)}, f32[2,512,512]{2,1,0:T(8,128)}, u32[]{:S(2)}, u32[]{:S(2)}) %collective-permute-start.5) | collective-permute-done | bytes 2097184 | tf_op jit(solution)/shard_map/ppermute | solution.py:32
  136.9 46.5 %collective-permute-done.6 = f32[2,512,512]{2,1,0:T(8,128)} collective-permute-done((f32[2,512,512]{2,1,0:T(8,128)}, f32[2,512,512]{2,1,0:T(8,128)}, u32[]{:S(2)}, u32[]{:S(2)}) %collective-permute-start.6) | collective-permute-done | bytes 2097184 | tf_op jit(solution)/shard_map/ppermute | solution.py:32
  183.4 5.5 pad_maximum_fusion
  188.9 137.0 %while.25 = (s32[]{:T(128)}, f32[4,2,512,512]{3,2,1,0:T(8,128)}, s32[32,4]{0,1:T(4,128)S(1)}, f32[32,1,2,128,128]{4,3,0,2,1:T(8,128)}, s32[]{:T(128)}) while((s32[]{:T(128)}, f32[4,2,512,512]{3,2,1,0:T(8,128)}, s32[32,4]{0,1:T(4,128)S(1)}, f32[32,1,2,128,128]{4,3,0,2,1:T(8,128)}, s32[]{:T(128)}) %tuple.106), condition=%wide.while_cond.9, body=%wide.while_body.9.sunk | while | flops 2 | bytes 264313 | solution.py:75
  351.2 4.0 fusion.30
  381.5 4.0 subtract_multiply_fusion
  385.5 4.7 add_bitcast_fusion
  394.1 6.1 broadcast_in_dim.10
  400.2 264.3 %while.24 = (s32[]{:T(128)}, f32[4,3,512,512]{3,2,1,0:T(8,128)}, s32[8,4]{0,1:T(4,128)S(1)}, s32[8,2]{0,1:T(2,128)S(1)}, f32[8,4,3,128,128]{4,3,2,1,0:T(8,128)},...) while((s32[]{:T(128)}, f32[4,3,512,512]{3,2,1,0:T(8,128)}, s32[8,4]{0,1:T(4,128)S(1)}, ...), condition=%wide.region_2.3_spmd, body=%wide.region_1.2_spmd.sunk | while | flops 196628 | bytes 3932589 | solution.py:114
  407.9 4.0 dynamic_update_slice.32
  414.8 4.0 dynamic_update_slice.33
  429.2 4.0 dynamic_update_slice.35
  440.9 4.0 dynamic_update_slice.32
  447.9 4.1 dynamic_update_slice.33
  455.1 4.1 dynamic_update_slice.34
  462.5 4.0 dynamic_update_slice.35
  474.2 4.0 dynamic_update_slice.32
  481.1 4.0 dynamic_update_slice.33
  495.6 4.0 dynamic_update_slice.35
  521.3 4.0 dynamic_update_slice.34
  528.6 4.0 dynamic_update_slice.35
  540.4 4.0 dynamic_update_slice.32
  547.3 4.1 dynamic_update_slice.33
  554.5 4.0 dynamic_update_slice.34
  561.9 4.0 dynamic_update_slice.35
  573.6 4.1 dynamic_update_slice.32
  580.6 4.1 dynamic_update_slice.33
  587.9 4.0 dynamic_update_slice.34
  595.2 4.1 dynamic_update_slice.35
  607.1 4.0 dynamic_update_slice.32
  614.0 4.0 dynamic_update_slice.33
  621.1 4.0 dynamic_update_slice.34
  628.4 4.0 dynamic_update_slice.35
  668.3 66.9 %collective-permute-done.7 = f32[3,512,512]{2,1,0:T(8,128)S(1)} collective-permute-done((f32[3,512,512]{2,1,0:T(8,128)S(1)}, f32[3,512,512]{2,1,0:T(8,128)S(1)}, u32[]{:S(2)}, u32[]{:S(2)}) %collective-permute-start.7) | collective-permute-done | bytes 3145760 | tf_op jit(solution)/shard_map/ppermute | solution.py:32
  737.8 5.9 collective-permute-start.8
  743.7 66.1 %collective-permute-done.8 = f32[3,512,512]{2,1,0:T(8,128)S(1)} collective-permute-done((f32[3,512,512]{2,1,0:T(8,128)S(1)}, f32[3,512,512]{2,1,0:T(8,128)S(1)}, u32[]{:S(2)}, u32[]{:S(2)}) %collective-permute-start.8) | collective-permute-done | bytes 3145760 | tf_op jit(solution)/shard_map/ppermute | solution.py:32
  810.5 5.9 collective-permute-start.9
  816.4 65.2 %collective-permute-done.9 = f32[3,512,512]{2,1,0:T(8,128)S(1)} collective-permute-done((f32[3,512,512]{2,1,0:T(8,128)S(1)}, f32[3,512,512]{2,1,0:T(8,128)S(1)}, u32[]{:S(2)}, u32[]{:S(2)}) %collective-permute-start.9) | collective-permute-done | bytes 3145760 | tf_op jit(solution)/shard_map/ppermute | solution.py:32
  882.5 7.7 collective-permute-start.10
  895.5 7.4 collective-permute-done.11
  906.9 9.3 collective-permute-start.12
  938.6 4.6 scatter-add.30
  959.7 6.4 scatter-add.34
  (256 shorter events, 348.7 us)
Async XLA Ops:
  1.1 7.7 collective-permute-start
  3.6 11.0 %collective-permute-start.1 = (f32[2,64,384]{2,1,0:T(8,128)S(1)}, f32[2,64,384]{2,1,0:T(8,128)S(1)}, u32[]{:S(2)}, u32[]{:S(2)}) collective-permute-start(f32[2,64,384]{2,1,0:T(8,128)S(1)} %get-tuple-element.283), channel_id=1, source_target_pairs={{16,0},{32,16},{48,32},{64,48},{80,64},{96,80},{112,96},{17,1},{33... | collective-permute-start | bytes 589832 | tf_op jit(solution)/shard_map/ppermute | solution.py:25
  14.9 11.8 %collective-permute-start.2 = (f32[2,512,64]{2,1,0:T(8,128)S(1)}, f32[2,512,64]{2,1,0:T(8,128)S(1)}, u32[]{:S(2)}, u32[]{:S(2)}) collective-permute-start(f32[2,512,64]{2,1,0:T(8,128)S(1)} %get-tuple-element.281), channel_id=1, source_target_pairs={{0,1},{1,2},{2,3},{3,4},{4,5},{5,6},{6,7},{7,8},{8,9},{9,10},{10,1... | collective-permute-start | bytes 786440 | tf_op jit(solution)/shard_map/ppermute | solution.py:22
  20.5 112.0 %copy-start.11 = (s32[1,1,8,2]{2,3,1,0:T(2,128)S(1)}, s32[1,1,8,2]{2,3,1,0:T(2,128)}, u32[]{:S(2)}) copy-start(s32[1,1,8,2]{2,3,1,0:T(2,128)} %param.30) | copy-start | bytes 196
  20.5 112.0 %copy-start.10 = (s32[8,4]{0,1:T(4,128)S(1)}, s32[8,4]{0,1:T(4,128)}, u32[]{:S(2)}) copy-start(s32[8,4]{0,1:T(4,128)} %param.32) | copy-start | bytes 388
  20.5 112.9 %copy-start.4 = (f32[4,2,128,128]{3,2,1,0:T(8,128)S(1)}, f32[4,2,128,128]{3,2,1,0:T(8,128)}, u32[]{:S(2)}) copy-start(f32[4,2,128,128]{3,2,1,0:T(8,128)} %param.29) | copy-start | bytes 1572868
  20.5 11.6 %collective-permute-start.3 = (f32[2,512,64]{2,1,0:T(8,128)S(1)}, f32[2,512,64]{2,1,0:T(8,128)S(1)}, u32[]{:S(2)}, u32[]{:S(2)}) collective-permute-start(f32[2,512,64]{2,1,0:T(8,128)S(1)} %get-tuple-element.282), channel_id=1, source_target_pairs={{1,0},{2,1},{3,2},{4,3},{5,4},{6,5},{7,6},{8,7},{9,8},{10,9},{11,1... | collective-permute-start | bytes 786440 | tf_op jit(solution)/shard_map/ppermute | solution.py:25
  32.8 48.5 %collective-permute-start.4 = (f32[2,512,512]{2,1,0:T(8,128)S(1)}, f32[2,512,512]{2,1,0:T(8,128)S(1)}, u32[]{:S(2)}, u32[]{:S(2)}) collective-permute-start(f32[2,512,512]{2,1,0:T(8,128)S(1)} %pad_maximum_fusion.2), channel_id=1, source_target_pairs={{0,112},{16,0},{32,16},{48,32},{64,48},{80,64},{96,80},{112,96},{1... | collective-permute-start | bytes 6291464 | tf_op jit(solution)/shard_map/ppermute | solution.py:32
  81.3 1.4 copy-start.5
  82.7 49.7 %collective-permute-start.5 = (f32[2,512,512]{2,1,0:T(8,128)S(1)}, f32[2,512,512]{2,1,0:T(8,128)}, u32[]{:S(2)}, u32[]{:S(2)}) collective-permute-start(f32[2,512,512]{2,1,0:T(8,128)S(1)} %collective-permute-done.4), channel_id=1, source_target_pairs={{0,112},{16,0},{32,16},{48,32},{64,48},{80,64},{96,80},{112,96},{1... | collective-permute-start | bytes 6291464 | tf_op jit(solution)/shard_map/ppermute | solution.py:32
  132.4 51.1 %collective-permute-start.6 = (f32[2,512,512]{2,1,0:T(8,128)}, f32[2,512,512]{2,1,0:T(8,128)}, u32[]{:S(2)}, u32[]{:S(2)}) collective-permute-start(f32[2,512,512]{2,1,0:T(8,128)} %collective-permute-done.5), channel_id=1, source_target_pairs={{0,112},{16,0},{32,16},{48,32},{64,48},{80,64},{96,80},{112,96},{1... | collective-permute-start | bytes 6291464 | tf_op jit(solution)/shard_map/ppermute | solution.py:32
  136.1 47.3 %copy-start.6 = (f32[2,512,512]{2,1,0:T(8,128)S(1)}, f32[2,512,512]{2,1,0:T(8,128)}, u32[]{:S(2)}) copy-start(f32[2,512,512]{2,1,0:T(8,128)} %copy-done.5) | copy-start | bytes 6291460
  355.2 3.8 copy-start.8
  385.5 4.7 copy-start.2
  664.5 145.3 %copy-start = (f32[4,3,512,512]{3,2,1,0:T(8,128)S(1)}, f32[4,3,512,512]{3,2,1,0:T(8,128)}, u32[]{:S(2)}) copy-start(f32[4,3,512,512]{3,2,1,0:T(8,128)} %get-tuple-element.215) | copy-start | bytes 37748740
  666.9 68.3 %collective-permute-start.7 = (f32[3,512,512]{2,1,0:T(8,128)S(1)}, f32[3,512,512]{2,1,0:T(8,128)S(1)}, u32[]{:S(2)}, u32[]{:S(2)}) collective-permute-start(f32[3,512,512]{2,1,0:T(8,128)S(1)} %slice_bitcast_fusion), channel_id=1, source_target_pairs={{0,16},{16,32},{32,48},{48,64},{64,80},{80,96},{96,112},{112,0},{1... | collective-permute-start | bytes 9437192 | tf_op jit(solution)/shard_map/ppermute | solution.py:32
  737.8 72.0 %collective-permute-start.8 = (f32[3,512,512]{2,1,0:T(8,128)S(1)}, f32[3,512,512]{2,1,0:T(8,128)S(1)}, u32[]{:S(2)}, u32[]{:S(2)}) collective-permute-start(f32[3,512,512]{2,1,0:T(8,128)S(1)} %bitcast_add_fusion.6), channel_id=1, source_target_pairs={{0,16},{16,32},{32,48},{48,64},{64,80},{80,96},{96,112},{112,0},{1... | collective-permute-start | bytes 9437192 | tf_op jit(solution)/shard_map/ppermute | solution.py:32
  810.5 71.1 %collective-permute-start.9 = (f32[3,512,512]{2,1,0:T(8,128)S(1)}, f32[3,512,512]{2,1,0:T(8,128)S(1)}, u32[]{:S(2)}, u32[]{:S(2)}) collective-permute-start(f32[3,512,512]{2,1,0:T(8,128)S(1)} %bitcast_add_fusion.5), channel_id=1, source_target_pairs={{0,16},{16,32},{32,48},{48,64},{64,80},{80,96},{96,112},{112,0},{1... | collective-permute-start | bytes 9437192 | tf_op jit(solution)/shard_map/ppermute | solution.py:32
  882.5 13.1 %collective-permute-start.10 = (f32[3,64,512]{2,1,0:T(8,128)S(1)}, f32[3,64,512]{2,1,0:T(8,128)S(1)}, u32[]{:S(2)}, u32[]{:S(2)}) collective-permute-start(f32[3,64,512]{2,1,0:T(8,128)S(1)} %get-tuple-element.279), channel_id=1, source_target_pairs={{0,16},{16,32},{32,48},{48,64},{64,80},{80,96},{96,112},{1,17},{17... | collective-permute-start | bytes 1179656 | tf_op jit(solution)/shard_map/ppermute | solution.py:22
  890.2 12.8 %collective-permute-start.11 = (f32[3,64,512]{2,1,0:T(8,128)S(1)}, f32[3,64,512]{2,1,0:T(8,128)S(1)}, u32[]{:S(2)}, u32[]{:S(2)}) collective-permute-start(f32[3,64,512]{2,1,0:T(8,128)S(1)} %get-tuple-element.280), channel_id=1, source_target_pairs={{16,0},{32,16},{48,32},{64,48},{80,64},{96,80},{112,96},{17,1},{33... | collective-permute-start | bytes 1179656 | tf_op jit(solution)/shard_map/ppermute | solution.py:25
  895.5 9.1 copy-start.7
  904.6 16.5 %copy-start.12 = (s32[3]{0:T(128)S(1)}, s32[3]{0:T(128)}, u32[]{:S(2)}) copy-start(s32[3]{0:T(128)} %constant.332.clone.1) | copy-start | bytes 40
  906.9 15.4 %collective-permute-start.12 = (f32[3,640,64]{1,2,0:T(8,128)}, f32[3,640,64]{1,2,0:T(8,128)}, u32[]{:S(2)}, u32[]{:S(2)}) collective-permute-start(f32[3,640,64]{1,2,0:T(8,128)} %copy.93), channel_id=1, source_target_pairs={{0,1},{1,2},{2,3},{3,4},{4,5},{5,6},{6,7},{7,8},{8,9},{9,10},{10,1... | collective-permute-start | bytes 1474568 | tf_op jit(solution)/shard_map/ppermute | solution.py:22
  918.6 11.4 %collective-permute-start.13 = (f32[3,640,64]{1,2,0:T(8,128)}, f32[3,640,64]{1,2,0:T(8,128)}, u32[]{:S(2)}, u32[]{:S(2)}) collective-permute-start(f32[3,640,64]{1,2,0:T(8,128)} %copy.95), channel_id=1, source_target_pairs={{1,0},{2,1},{3,2},{4,3},{5,4},{6,5},{7,6},{8,7},{9,8},{10,9},{11,1... | collective-permute-start | bytes 1474568 | tf_op jit(solution)/shard_map/ppermute | solution.py:25
  956.0 3.6 copy-start.1
  957.1 11.6 %copy-start.9 = (f32[3,64,64]{1,2,0:T(8,128)S(1)}, f32[3,64,64]{1,2,0:T(8,128)}, u32[]{:S(2)}) copy-start(f32[3,64,64]{1,2,0:T(8,128)} %get-tuple-element.287) | copy-start | bytes 147460
  966.0 4.8 copy-start.3
where the time goes:
time: 988 us; the launch traced here: 972 us
  waiting for transfers between devices  373 us (38%)
  local copies, waits for them, and re-layouts  325 us (33%)
  loops' own time  91.6 us (9%)
  other arithmetic  73.3 us (7%)
  matrix products  61 us (6%)
  starting transfers between devices  47 us (5%)
    ppermute x6, waiting for transfers between devices, shifted(): return lax.ppermute(x, axis, [(i, (i + by) % peers) for i in range(peers)])  343 us
    gather x96, local copies, waits for them, and re-layouts  137 us
    dynamic_update_slice x32, local copies, waits for them, and re-layouts, add_scan(): lax.dynamic_update_slice(accum, current + contrib[slot, beam][None], start)  127 us
    another operation x1, loops' own time, on_device(): accum = lax.fori_loop(0, SCANS, add_scan, accum)  91.4 us
    add x32, other arithmetic, add_scan(): current + contrib[slot, beam][None]  40 us
    ppermute x4, starting transfers between devices, extended(): lax.ppermute(lax.slice_in_dim(block, block.shape[dim] - width, None, axis...  25.2 us
    scatter-add x7, local copies, waits for them, and re-layouts, on_device(): interior.at[:, row_dst:row_dst + row_len, col_dst:col_dst + col_len]  20.7 us
  transfers between devices with their start and end apart: 14, of which 14 were waited for; matrix products, arithmetic and copies ran while one was open for 1% of the time, Pallas kernels for 0%

commit v1 on v0

v1 whole, which is shorter than its diff:
```python
import functools
import math

import jax
import jax.numpy as jnp
import numpy as np
from jax import lax
from jax.experimental import pallas as pl
from jax.experimental.pallas import tpu as pltpu
from jax.sharding import PartitionSpec as P

SIDE = 128
HALF = 64
BEAMS = 4
SCANS = 8
TILE = 384
TALL = TILE + 2 * HALF
COLUMNS = TILE // SIDE
SLABS = COLUMNS + 2
EPSILON = 0.5
DAMPING = 0.5
MESH = pl.DeviceIdType.MESH
VMEM = pl.BlockSpec(memory_space=pltpu.VMEM)
SMEM = pl.BlockSpec(memory_space=pltpu.SMEM)


def tables():
    index = np.arange(SIDE)
    angle = (index[:, None] * index[None, :] % SIDE) * (2.0 * math.pi / SIDE)
    c = np.cos(angle) / math.sqrt(SIDE)
    s = np.sin(angle) / math.sqrt(SIDE)
    lane = np.block([[c, -s], [s, c]])
    both = np.stack([lane, lane.T]).astype(np.float32)
    high = both.astype(jnp.bfloat16)
    low = (both - high.astype(np.float32)).astype(jnp.bfloat16)
    return high, low


def greet(partners):
    barrier = pltpu.get_barrier_semaphore()
    for partner in partners:
        pl.semaphore_signal(barrier, inc=1, device_id=partner, device_id_type=MESH)
    pl.semaphore_wait(barrier, len(partners))


def split(x):
    high = x.astype(jnp.bfloat16)
    return high, (x - high.astype(jnp.float32)).astype(jnp.bfloat16)


def dot(a, b):
    return jnp.dot(a, b, preferred_element_type=jnp.float32)


def on_lanes(x, high, low):
    x_high, x_low = split(x)
    return dot(x_high, high) + (dot(x_low, high) + dot(x_high, low))


def on_rows(high, low, x):
    x_high, x_low = split(x)
    return dot(high, x_high) + (dot(high, x_low) + dot(low, x_high))


def lane_start(x):
    at = x + HALF
    slab = lax.div(at, SIDE)
    return slab, at - slab * SIDE


def neighbours(i, j, nr, nc):
    up, down = lax.rem(i + nr - 1, nr), lax.rem(i + 1, nr)
    left, right = lax.rem(j + nc - 1, nc), lax.rem(j + 1, nc)
    return up, down, left, right


def frame_kernel(nr, nc, obj, meta, frame, metas, pack, send, recv):
    i, j = lax.axis_index("row"), lax.axis_index("col")
    up, down, left, right = neighbours(i, j, nr, nc)
    later = [lax.rem(i + k, nr) for k in (1, 2, 3)]
    earlier = [lax.rem(i + nr - k, nr) for k in (1, 2, 3)]
    lane = lax.broadcasted_iota(jnp.int32, (TILE, SIDE), 1)
    last = TILE - SIDE
    pack[0] = jnp.where(lane < HALF, obj[0, :, 0:SIDE], pltpu.roll(obj[1, :, 0:SIDE], HALF, 1))
    pack[1] = jnp.where(lane < HALF, pltpu.roll(obj[1, :, last:TILE], HALF, 1), obj[0, :, last:TILE])
    metas[0] = meta[...]
    greet(
        [{"row": r} for r in later + earlier]
        + [{"col": left}, {"col": right}]
        + [{"row": r, "col": c} for r in (up, down) for c in (left, right)]
    )
    top, low_edge, end = TILE - HALF, HALF + TILE, SLABS - 1
    plan = [
        (pack.at[0], frame.at[0, end, HALF:low_edge], {"col": left}),
        (pack.at[1], frame.at[0, 0, HALF:low_edge], {"col": right}),
        (pack.at[0, 0:HALF], frame.at[0, end, low_edge:TALL], {"row": up, "col": left}),
        (pack.at[0, top:TILE], frame.at[0, end, 0:HALF], {"row": down, "col": left}),
        (pack.at[1, 0:HALF], frame.at[0, 0, low_edge:TALL], {"row": up, "col": right}),
        (pack.at[1, top:TILE], frame.at[0, 0, 0:HALF], {"row": down, "col": right}),
    ] + [(meta, metas.at[k + 1], {"row": later[k]}) for k in range(3)]
    for b in range(COLUMNS):
        part = slice(b * SIDE, (b + 1) * SIDE)
        plan.append((obj.at[:, 0:HALF, part], frame.at[:, b + 1, low_edge:TALL], {"row": up}))
        plan.append((obj.at[:, top:TILE, part], frame.at[:, b + 1, 0:HALF], {"row": down}))
    copies = [
        pltpu.make_async_remote_copy(
            src_ref=src, dst_ref=dst, send_sem=send.at[q], recv_sem=recv.at[q], device_id=to, device_id_type=MESH
        )
        for q, (src, dst, to) in enumerate(plan)
    ]
    for copy in copies:
        copy.start()
    for b in range(COLUMNS):
        frame[:, b + 1, HALF:low_edge] = obj[:, :, b * SIDE : (b + 1) * SIDE]
    for copy in copies:
        copy.wait()
    for slab in (0, end):
        frame[1, slab] = pltpu.roll(frame[0, slab], HALF, 1)

    @pl.when(i == 0)
    def _():
        frame[:, :, 0:HALF] = jnp.zeros((2, SLABS, HALF, SIDE), jnp.float32)

    @pl.when(i == nr - 1)
    def _():
        frame[:, :, low_edge:TALL] = jnp.zeros((2, SLABS, HALF, SIDE), jnp.float32)

    @pl.when(j == 0)
    def _():
        frame[:, 0] = jnp.zeros((2, TALL, SIDE), jnp.float32)

    @pl.when(j == nc - 1)
    def _():
        frame[:, end] = jnp.zeros((2, TALL, SIDE), jnp.float32)


def wave_kernel(nr, frame, probe, metas, offsets, measured, high, low, grads, psi, far, inten, relay, gathered, facs, send, recv):
    me = lax.axis_index("row")

    def to(by):
        return {"row": lax.rem(me + by + nr, nr)}

    greet([to(1), to(-1), to(3), to(-3)])

    def beam_at(s, k):
        beam = jnp.int32(0)
        for q in range(1, BEAMS):
            beam = jnp.where(offsets[s, q] == k, q, beam)
        return beam

    def copy(s, kind):
        odd = lax.rem(s, 2)
        near = 1 + 2 * odd
        straight = 3 - 2 * odd
        if kind == 0:
            src, dst, dev = inten.at[s, 2], relay.at[s], to(2 * odd - 1)
        elif kind == 1:
            src, dst, dev = inten.at[s, straight], gathered.at[s, 0], to(-straight)
        elif kind == 2:
            src, dst, dev = inten.at[s, near], gathered.at[s, 1], to(-near)
        elif kind == 3:
            src, dst, dev = facs.at[s, 0], facs.at[s, near], to(near)
        elif kind == 4:
            src, dst, dev = facs.at[s, 0], facs.at[s, straight], to(straight)
        else:
            src, dst, dev = facs.at[s, near], facs.at[s, 2], to(1 - 2 * odd)
        return pltpu.make_async_remote_copy(
            src_ref=src,
            dst_ref=dst,
            send_sem=send.at[s, kind],
            recv_sem=recv.at[s, kind],
            device_id=dev,
            device_id_type=MESH,
        )

    column = lax.broadcasted_iota(jnp.int32, (SIDE, SIDE), 1)

    def forward(s):
        rows = []
        for k in range(BEAMS):
            y = metas[k, s, 0]
            slab, lane = lane_start(metas[k, s, 1])
            turn = lax.rem(SIDE - lane, SIDE)
            beam = beam_at(s, k)
            z_re, z_im = [
                jnp.where(
                    column < SIDE - lane,
                    pltpu.roll(frame[c, slab, pl.ds(y, SIDE)], turn, 1),
                    pltpu.roll(frame[c, slab + 1, pl.ds(y, SIDE)], turn, 1),
                )
                for c in range(2)
            ]
            p_re, p_im = probe[beam, 0], probe[beam, 1]
            wave = jnp.concatenate([p_re * z_re - p_im * z_im, p_re * z_im + p_im * z_re], axis=1)
            psi[s, k * SIDE : (k + 1) * SIDE] = wave
            rows.append(wave)
        once = on_lanes(jnp.concatenate(rows, axis=0), high[0], low[0])
        once = jnp.concatenate(
            [
                jnp.concatenate([once[k * SIDE : (k + 1) * SIDE, q * SIDE : (q + 1) * SIDE] for k in range(BEAMS)], axis=1)
                for q in range(2)
            ],
            axis=0,
        )
        twice = on_rows(high[1], low[1], once)
        far[s] = twice
        for k in range(BEAMS):
            re = twice[:SIDE, k * SIDE : (k + 1) * SIDE]
            im = twice[SIDE:, k * SIDE : (k + 1) * SIDE]
            inten[s, k] = re * re + im * im
        copy(s, 0).start()
        copy(s, 1).start()

    def join(s):
        copy(s, 0).wait_recv()
        near = 1 + 2 * lax.rem(s, 2)
        inten[s, near] = inten[s, near] + relay[s]
        copy(s, 2).start()

    def settle(s):
        copy(s, 1).wait_recv()
        copy(s, 2).wait_recv()
        total = inten[s, 0] + gathered[s, 0] + gathered[s, 1]
        facs[s, 0] = measured[s] / jnp.sqrt(total + EPSILON)
        copy(s, 3).start()
        copy(s, 4).start()

    def hand_on(s):
        copy(s, 3).wait_recv()
        copy(s, 5).start()

    def back(s):
        copy(s, 4).wait_recv()
        copy(s, 5).wait_recv()
        factor = jnp.concatenate([facs[s, k] for k in range(BEAMS)], axis=1)
        scaled = jnp.concatenate([far[s, :SIDE] * factor, far[s, SIDE:] * factor], axis=0)
        once = on_rows(high[0], low[0], scaled)
        once = jnp.concatenate(
            [
                jnp.concatenate([once[q * SIDE : (q + 1) * SIDE, k * SIDE : (k + 1) * SIDE] for q in range(2)], axis=1)
                for k in range(BEAMS)
            ],
            axis=0,
        )
        change = on_lanes(once, high[1], low[1]) - psi[s]
        for k in range(BEAMS):
            beam = beam_at(s, k)
            p_re, p_im = probe[beam, 0], probe[beam, 1]
            c_re = change[k * SIDE : (k + 1) * SIDE, :SIDE]
            c_im = change[k * SIDE : (k + 1) * SIDE, SIDE:]
            grads[s, k * SIDE : (k + 1) * SIDE, :SIDE] = p_re * c_re + p_im * c_im
            grads[s, k * SIDE : (k + 1) * SIDE, SIDE:] = p_re * c_im - p_im * c_re

    stages = ((forward, 0), (join, 1), (settle, 2), (hand_on, 3), (back, 4))

    def step(t, carry):
        for stage, lag in stages:

            @pl.when(jnp.logical_and(t >= lag, t < SCANS + lag))
            def _(stage=stage, lag=lag):
                stage(t - lag)

        return carry

    lax.fori_loop(0, SCANS + stages[-1][1], step, 0)

    def drain(s, carry):
        for kind in range(6):
            copy(s, kind).wait_send()
        return carry

    lax.fori_loop(0, SCANS, drain, 0)


def place_kernel(grads, probe, metas, offsets, accum, illum):
    for b in range(BEAMS):
        illum[b] = probe[b, 0] * probe[b, 0] + probe[b, 1] * probe[b, 1]
    accum[...] = jnp.zeros_like(accum)
    column = lax.broadcasted_iota(jnp.int32, (SIDE, SIDE), 1)

    def add_one(q, carry):
        s, k = lax.div(q, BEAMS), lax.rem(q, BEAMS)

        @pl.when(s < metas[k, 0, 2])
        def _():
            y = metas[k, s, 0]
            slab, lane = lane_start(metas[k, s, 1])
            beam = jnp.int32(0)
            for b in range(1, BEAMS):
                beam = jnp.where(offsets[s, b] == k, b, beam)
            at = pl.ds(pl.multiple_of(k * SIDE, SIDE), SIDE)
            parts = (grads[s, at, :SIDE], grads[s, at, SIDE:], illum[beam])
            for channel, part in enumerate(parts):
                turned = pltpu.roll(part, lane, 1)
                here, there = (channel, slab, pl.ds(y, SIDE)), (channel, slab + 1, pl.ds(y, SIDE))
                accum[here] = accum[here] + jnp.where(column >= lane, turned, 0.0)
                accum[there] = accum[there] + jnp.where(column < lane, turned, 0.0)

        return carry

    lax.fori_loop(0, SCANS * BEAMS, add_one, 0)


def rim_kernel(nr, nc, accum, obj, out, pack, rows_in, sides_in, weights_in, send, recv):
    i, j = lax.axis_index("row"), lax.axis_index("col")
    up, down, left, right = neighbours(i, j, nr, nc)
    low_edge, top, end = HALF + TILE, TILE - HALF, SLABS - 1
    lane = lax.broadcasted_iota(jnp.int32, (TALL, SIDE), 1)
    pack[0] = jnp.where(lane >= HALF, accum[0, 0], pltpu.roll(accum[1, 0], HALF, 1))
    pack[1] = jnp.where(lane < HALF, accum[0, end], pltpu.roll(accum[1, end], HALF, 1))
    greet(
        [{"row": up}, {"row": down}, {"col": left}, {"col": right}]
        + [{"row": r, "col": c} for r in (up, down) for c in (left, right)]
    )
    plan = [
        (accum.at[:, 1:end, 0:HALF], rows_in.at[1], {"row": up}),
        (accum.at[:, 1:end, low_edge:TALL], rows_in.at[0], {"row": down}),
    ]
    ends = ((0, HALF, low_edge, up), (HALF, low_edge, HALF, None), (low_edge, TALL, 0, down))
    for side, (slab, to_col) in enumerate(((0, left), (end, right))):
        for first, stop, land, to_row in ends:
            to = {"col": to_col} if to_row is None else {"row": to_row, "col": to_col}
            arrive = slice(land, land + stop - first)
            plan.append((pack.at[side, first:stop], sides_in.at[side, arrive], to))
            plan.append((accum.at[2, slab, first:stop], weights_in.at[side, arrive], to))
    copies = [
        pltpu.make_async_remote_copy(
            src_ref=src, dst_ref=dst, send_sem=send.at[q], recv_sem=recv.at[q], device_id=to, device_id_type=MESH
        )
        for q, (src, dst, to) in enumerate(plan)
    ]
    for copy in copies:
        copy.start()
    for copy in copies:
        copy.wait()

    def kept(ok, value):
        return jnp.where(ok, value, 0.0)

    lane = lax.broadcasted_iota(jnp.int32, (TILE, SIDE), 1)

    def gather(head, middle, tail):
        return jnp.concatenate([head, middle, tail], axis=0)

    def column(ref, side):
        head = ref[side, HALF:SIDE] + kept(i > 0, ref[side, 0:HALF])
        tail = ref[side, TILE:low_edge] + kept(i < nr - 1, ref[side, low_edge:TALL])
        return gather(head, ref[side, SIDE:TILE], tail)

    from_right, from_left = column(sides_in, 0), column(sides_in, 1)
    rights = (from_right, pltpu.roll(from_right, HALF, 1), column(weights_in, 0))
    lefts = (from_left, pltpu.roll(from_left, HALF, 1), column(weights_in, 1))
    for b in range(COLUMNS):
        sums = []
        for c in range(3):
            head = accum[c, b + 1, HALF:SIDE] + kept(i > 0, rows_in[0, c, b])
            tail = accum[c, b + 1, TILE:low_edge] + kept(i < nr - 1, rows_in[1, c, b])
            value = gather(head, accum[c, b + 1, SIDE:TILE], tail)
            if b == 0:
                value = value + kept(jnp.logical_and(lane < HALF, j > 0), lefts[c])
            if b == COLUMNS - 1:
                value = value + kept(jnp.logical_and(lane >= HALF, j < nc - 1), rights[c])
            sums.append(value)
        part = slice(b * SIDE, (b + 1) * SIDE)
        for c in range(2):
            out[c, :, part] = obj[c, :, part] + sums[c] / (sums[2] + DAMPING)


def params(collective_id, mebibytes):
    return pltpu.CompilerParams(
        collective_id=collective_id, has_side_effects=True, vmem_limit_bytes=mebibytes * 2**20
    )


def f32(*shape):
    return jax.ShapeDtypeStruct(shape, jnp.float32)


def on_device(obj, probe, positions, counts, offsets, measured):
    nr, nc = lax.axis_size("row"), lax.axis_size("col")
    spots = positions[0, 0]
    count = jnp.broadcast_to(counts, (SCANS, 1))
    meta = jnp.pad(jnp.concatenate([spots, count], axis=1), ((0, 0), (0, SIDE - 3)))
    dma = pltpu.SemaphoreType.DMA
    frame, metas = pl.pallas_call(
        functools.partial(frame_kernel, nr, nc),
        out_shape=(f32(2, SLABS, TALL, SIDE), jax.ShapeDtypeStruct((BEAMS, SCANS, SIDE), jnp.int32)),
        in_specs=[VMEM, VMEM],
        out_specs=(VMEM, VMEM),
        scratch_shapes=[pltpu.VMEM((2, TILE, SIDE), jnp.float32), dma((15,)), dma((15,))],
        compiler_params=params(1, 16),
        name="frame",
    )(obj, meta)
    high, low = tables()
    block = (SIDE, SIDE)
    grads = pl.pallas_call(
        functools.partial(wave_kernel, nr),
        out_shape=f32(SCANS, BEAMS * SIDE, 2 * SIDE),
        in_specs=[VMEM, VMEM, SMEM, SMEM, VMEM, VMEM, VMEM],
        out_specs=VMEM,
        scratch_shapes=[
            pltpu.VMEM((SCANS, BEAMS * SIDE, 2 * SIDE), jnp.float32),
            pltpu.VMEM((SCANS, 2 * SIDE, BEAMS * SIDE), jnp.float32),
            pltpu.VMEM((SCANS, BEAMS) + block, jnp.float32),
            pltpu.VMEM((SCANS,) + block, jnp.float32),
            pltpu.VMEM((SCANS, 2) + block, jnp.float32),
            pltpu.VMEM((SCANS, BEAMS) + block, jnp.float32),
            dma((SCANS, 6)),
            dma((SCANS, 6)),
        ],
        compiler_params=params(2, 40),
        name="wave",
    )(frame, probe, metas, offsets, measured[0, 0], jnp.asarray(high), jnp.asarray(low))
    accum = pl.pallas_call(
        place_kernel,
        out_shape=f32(3, SLABS, TALL, SIDE),
        in_specs=[VMEM, VMEM, SMEM, SMEM],
        out_specs=VMEM,
        scratch_shapes=[pltpu.VMEM((BEAMS,) + block, jnp.float32)],
        compiler_params=pltpu.CompilerParams(vmem_limit_bytes=24 * 2**20),
        name="place",
    )(grads, probe, metas, offsets)
    return pl.pallas_call(
        functools.partial(rim_kernel, nr, nc),
        out_shape=f32(2, TILE, TILE),
        in_specs=[VMEM, VMEM],
        out_specs=VMEM,
        scratch_shapes=[
            pltpu.VMEM((2, TALL, SIDE), jnp.float32),
            pltpu.VMEM((2, 3, COLUMNS, HALF, SIDE), jnp.float32),
            pltpu.VMEM((2, TALL, SIDE), jnp.float32),
            pltpu.VMEM((2, TALL, SIDE), jnp.float32),
            dma((14,)),
            dma((14,)),
        ],
        compiler_params=params(3, 24),
        name="rim",
    )(accum, obj)


def solution(mesh):
    return jax.shard_map(
        on_device,
        mesh=mesh,
        in_specs=(
            P(None, "row", "col"),
            P(),
            P("row", "col", None, None),
            P("row", "col"),
            P(),
            P("row", "col", None, None, None),
        ),
        out_specs=P(None, "row", "col"),
        check_vma=False,
    )
```

time: 988 us -> 118 us (0.12)
  the two profiles are of different devices: /device:TPU:105 before, /device:TPU:13 now
where the time goes in v1:
time: 118 us; the launch traced here: 116 us
  Pallas kernels  107 us (91%)
  local copies, waits for them, and re-layouts  7.78 us (7%)
    pallas_call x1, Pallas kernels, on_device(): pl.pallas_call(functools.partial(wave_kernel, nr), out_shape=f32(SCANS, B...  52.6 us
    pallas_call x1, Pallas kernels, on_device(): pl.pallas_call(functools.partial(rim_kernel, nr, nc), out_shape=f32(2, TI...  33.9 us
    pallas_call x1, Pallas kernels, on_device(): pl.pallas_call(functools.partial(frame_kernel, nr, nc), out_shape=(f32(2,...  16.7 us
    unnamed x14, local copies, waits for them, and re-layouts  7.03 us
    pallas_call x1, Pallas kernels, on_device(): pl.pallas_call(place_kernel, out_shape=f32(3, SLABS, TALL, SIDE), in_spec...  4.26 us

profile of v1, /device:TPU:13, one launch (start us, length us, event | category | flops | bytes accessed | tf_op | source)
XLA Modules:
  0.0 116.0 jit_solution(5023536026604740568)
XLA Ops:
  0.7 0.8 copy.10.offsets
  1.4 0.8 copy.9
  2.2 0.0 copy-start
  2.2 1.3 %copy-done = f32[2,384,384]{2,1,0:T(8,128)S(1)} copy-done((f32[2,384,384]{2,1,0:T(8,128)S(1)}, f32[2,384,384]{2,1,0:T(8,128)}, u32[]{:S(2)}) %copy-start) | copy-done | bytes 1179672
  3.4 16.7 %frame.1 = (f32[2,5,512,128]{3,2,1,0:T(8,128)S(1)}, s32[4,8,128]{2,1,0:T(8,128)S(1)}) custom-call(f32[2,384,384]{2,1,0:T(8,128)S(1)} %copy-done, s32[8,128]{1,0:T(8,128)S(1)} %pad_select_fusion.meta), custom_call_target="tpu_custom_call" | custom-call | tf_op jit(solution)/shard_map/frame/pallas_call | solution.py:385
  20.1 0.0 copy-start.2
  20.1 1.0 copy-done.2
  21.2 0.0 copy-start.3
  21.2 1.0 copy-done.3
  22.2 0.0 copy-start.4
  22.2 0.9 copy-done.4
  23.1 0.0 copy-start.5
  23.2 0.9 copy-done.5
  24.1 52.6 %wave.1.grads = f32[8,512,256]{2,1,0:T(8,128)S(1)} custom-call(f32[2,5,512,128]{3,2,1,0:T(8,128)S(1)} %get-tuple-element.7.frame, f32[4,2,128,128]{3,2,1,0:T(8,128)S(1)} %copy-done.2, s32[4,8,128]{2,1,0:T(8,128)S(1)} %get-tuple-element.8.metas, s32[8,4]{1,0:T(8,128)S(1)} %copy.10.offsets, f32[8,128,128]{2,1,0:T(8,128)S(1)} %bitcast.4, ...), custom_call_target="tpu_custom_call" | custom-call | tf_op jit(solution)/shard_map/wave/pallas_call | solution.py:396
  76.7 0.0 copy-start.1
  76.7 4.3 %place.1.accum = f32[3,5,512,128]{3,2,1,0:T(8,128)S(1)} custom-call(f32[8,512,256]{2,1,0:T(8,128)S(1)} %wave.1.grads, f32[4,2,128,128]{3,2,1,0:T(8,128)S(1)} %copy-done.2, s32[4,8,128]{2,1,0:T(8,128)S(1)} %get-tuple-element.8.metas, s32[8,4]{1,0:T(8,128)S(1)} %copy.10.offsets), custom_call_target="tpu_custom_call" | custom-call | tf_op jit(solution)/shard_map/place/pallas_call | solution.py:414
  81.0 0.0 copy-done.1
  81.0 33.9 %rim.1 = f32[2,384,384]{2,1,0:T(8,128)S(1)} custom-call(f32[3,5,512,128]{3,2,1,0:T(8,128)S(1)} %place.1.accum, f32[2,384,384]{2,1,0:T(8,128)S(1)} %copy-done.1), custom_call_target="tpu_custom_call" | custom-call | tf_op jit(solution)/shard_map/rim/pallas_call | solution.py:423
  115.0 1.0 copy.14
  (1 shorter events, 0.0 us)
Async XLA Ops:
  2.2 1.3 %copy-start = (f32[2,384,384]{2,1,0:T(8,128)S(1)}, f32[2,384,384]{2,1,0:T(8,128)}, u32[]{:S(2)}) copy-start(f32[2,384,384]{2,1,0:T(8,128)} %obj.3) | copy-start | bytes 3538948
  20.1 1.0 copy-start.2
  21.2 1.0 copy-start.3
  22.2 0.9 copy-start.4
  23.1 0.9 copy-start.5
  76.7 4.3 %copy-start.1 = (f32[2,384,384]{2,1,0:T(8,128)S(1)}, f32[2,384,384]{2,1,0:T(8,128)}, u32[]{:S(2)}) copy-start(f32[2,384,384]{2,1,0:T(8,128)} %obj.3) | copy-start | bytes 3538948

commit v2 on v1

v2 whole, which is shorter than its diff:
```python
import functools
import math

import jax
import jax.numpy as jnp
import numpy as np
from jax import lax
from jax.experimental import pallas as pl
from jax.experimental.pallas import tpu as pltpu
from jax.sharding import PartitionSpec as P

SIDE = 128
HALF = 64
BEAMS = 4
SCANS = 8
TILE = 384
TALL = TILE + 2 * HALF
COLUMNS = TILE // SIDE
SLABS = COLUMNS + 2
EPSILON = 0.5
DAMPING = 0.5
MESH = pl.DeviceIdType.MESH
VMEM = pl.BlockSpec(memory_space=pltpu.VMEM)
SMEM = pl.BlockSpec(memory_space=pltpu.SMEM)
ANY = pl.BlockSpec(memory_space=pl.ANY)
PAD = 512
STAGES = (("forward", 0), ("weigh", 2), ("join", 2), ("settle", 4), ("hand_on", 6), ("back", 8))
WEIGHTS_AT = 12


def tables():
    index = np.arange(SIDE)
    angle = (index[:, None] * index[None, :] % SIDE) * (2.0 * math.pi / SIDE)
    c = np.cos(angle) / math.sqrt(SIDE)
    s = np.sin(angle) / math.sqrt(SIDE)
    lane = np.block([[c, -s], [s, c]])
    both = np.stack([lane, lane.T]).astype(np.float32)
    high = both.astype(jnp.bfloat16)
    low = (both - high.astype(np.float32)).astype(jnp.bfloat16)
    return high, low


def split(x):
    high = x.astype(jnp.bfloat16)
    return high, (x - high.astype(jnp.float32)).astype(jnp.bfloat16)


def dot(a, b):
    return jnp.dot(a, b, preferred_element_type=jnp.float32)


def on_lanes(x, high, low):
    x_high, x_low = split(x)
    return dot(x_high, high) + (dot(x_low, high) + dot(x_high, low))


def on_rows(high, low, x):
    x_high, x_low = split(x)
    return dot(high, x_high) + (dot(high, x_low) + dot(low, x_high))


def lane_start(x):
    at = x + HALF
    slab = lax.div(at, SIDE)
    return slab, at - slab * SIDE


def ROUTE(z, s):
    return lax.rem(s, 2)


def neighbours(i, j, nr, nc):
    up, down = lax.rem(i + nr - 1, nr), lax.rem(i + 1, nr)
    left, right = lax.rem(j + nc - 1, nc), lax.rem(j + 1, nc)
    return up, down, left, right


def step_kernel(
    nr, nc, obj_hbm, probe_hbm, measured_hbm, high_hbm, low_hbm, meta, offsets, out,
    obj, probe, measured, high, low, metas_in, metas, frame, pack, psi, far, inten, relay, gathered, facs,
    padded, accum, rows_in, sides_in, weight_rows, weight_sides, local, send, recv, wave_send, wave_recv,
):
    i, j = lax.axis_index("row"), lax.axis_index("col")
    up, down, left, right = neighbours(i, j, nr, nc)
    later = [lax.rem(i + k, nr) for k in (1, 2, 3)]
    earlier = [lax.rem(i + nr - k, nr) for k in (1, 2, 3)]
    corners = [{"row": r, "col": c} for r in (up, down) for c in (left, right)]
    partners = [{"row": r} for r in later + earlier] + [{"col": left}, {"col": right}] + corners
    barrier = pltpu.get_barrier_semaphore()
    for partner in partners:
        pl.semaphore_signal(barrier, inc=1, device_id=partner, device_id_type=MESH)
    fetches = [
        pltpu.make_async_copy(src, dst, local.at[q])
        for q, (src, dst) in enumerate(
            ((obj_hbm, obj), (probe_hbm, probe), (high_hbm, high), (low_hbm, low), (measured_hbm, measured))
        )
    ]
    for fetch in fetches:
        fetch.start()
    metas_in[0] = meta[...]

    def clear(q, carry):
        padded[q] = jnp.zeros((2 * PAD, SIDE), jnp.float32)
        return carry

    lax.fori_loop(0, 4 * BEAMS + 1, clear, 0)

    def clear_sum(q, carry):
        accum[lax.div(q, SLABS), lax.rem(q, SLABS)] = jnp.zeros((TALL, SIDE), jnp.float32)
        return carry

    lax.fori_loop(0, 3 * SLABS, clear_sum, 0)
    fetches[0].wait()
    lane = lax.broadcasted_iota(jnp.int32, (TILE, SIDE), 1)
    low_edge, top, end, last = HALF + TILE, TILE - HALF, SLABS - 1, TILE - SIDE
    pack[0, HALF:low_edge] = jnp.where(lane < HALF, obj[0, :, 0:SIDE], pltpu.roll(obj[1, :, 0:SIDE], HALF, 1))
    pack[1, HALF:low_edge] = jnp.where(lane < HALF, pltpu.roll(obj[1, :, last:TILE], HALF, 1), obj[0, :, last:TILE])
    pl.semaphore_wait(barrier, len(partners))

    def exchange(plan, first):
        copies = [
            pltpu.make_async_remote_copy(
                src_ref=src,
                dst_ref=dst,
                send_sem=send.at[first + q],
                recv_sem=recv.at[first + q],
                device_id=dev,
                device_id_type=MESH,
            )
            for q, (src, dst, dev) in enumerate(plan)
        ]
        for one in copies:
            one.start()
        return copies

    heads, tails = slice(HALF, SIDE), slice(TILE, low_edge)
    plan = [(meta, metas_in.at[k + 1], {"row": later[k]}) for k in range(3)]
    for b in range(COLUMNS):
        part = slice(b * SIDE, (b + 1) * SIDE)
        plan.append((obj.at[:, 0:HALF, part], frame.at[:, b + 1, low_edge:TALL], {"row": up}))
        plan.append((obj.at[:, top:TILE, part], frame.at[:, b + 1, 0:HALF], {"row": down}))
    plan += [
        (pack.at[0, HALF:low_edge], frame.at[0, end, HALF:low_edge], {"col": left}),
        (pack.at[1, HALF:low_edge], frame.at[0, 0, HALF:low_edge], {"col": right}),
        (pack.at[0, heads], frame.at[0, end, low_edge:TALL], {"row": up, "col": left}),
        (pack.at[0, tails], frame.at[0, end, 0:HALF], {"row": down, "col": left}),
        (pack.at[1, heads], frame.at[0, 0, low_edge:TALL], {"row": up, "col": right}),
        (pack.at[1, tails], frame.at[0, 0, 0:HALF], {"row": down, "col": right}),
    ]
    copies = exchange(plan, 0)
    for b in range(COLUMNS):
        frame[:, b + 1, HALF:low_edge] = obj[:, :, b * SIDE : (b + 1) * SIDE]
    for fetch in fetches[1:]:
        fetch.wait()
    for one in copies[:3]:
        one.wait()
    settled = pltpu.make_async_copy(metas_in, metas, local.at[5])
    settled.start()
    for one in copies[3:]:
        one.wait()
    settled.wait()
    for slab in (0, end):
        frame[1, slab] = pltpu.roll(frame[0, slab], HALF, 1)

    @pl.when(i == 0)
    def _():
        frame[:, :, 0:HALF] = jnp.zeros((2, SLABS, HALF, SIDE), jnp.float32)

    @pl.when(i == nr - 1)
    def _():
        frame[:, :, low_edge:TALL] = jnp.zeros((2, SLABS, HALF, SIDE), jnp.float32)

    @pl.when(j == 0)
    def _():
        frame[:, 0] = jnp.zeros((2, TALL, SIDE), jnp.float32)

    @pl.when(j == nc - 1)
    def _():
        frame[:, end] = jnp.zeros((2, TALL, SIDE), jnp.float32)

    def to(by):
        return {"row": lax.rem(i + by + nr, nr)}

    def by_third(s, k):
        return ROUTE(lax.rem(i + nr - k, 4), s)

    def copy(s, kind):
        if kind == 0:
            src, dst, dev = inten.at[s, 2], relay.at[s, 0], to(-1)
        elif kind == 1:
            src, dst, dev = inten.at[s, 2], relay.at[s, 1], to(1)
        elif kind == 2:
            src, dst, dev = inten.at[s, 1], gathered.at[s, 0], to(-1)
        elif kind == 3:
            src, dst, dev = inten.at[s, 3], gathered.at[s, 1], to(-3)
        elif kind == 4:
            src, dst, dev = facs.at[s, 0], facs.at[s, 1], to(1)
        elif kind == 5:
            src, dst, dev = facs.at[s, 0], facs.at[s, 3], to(3)
        elif kind == 6:
            src, dst, dev = facs.at[s, 1], facs.at[s, 2], to(1)
        else:
            src, dst, dev = facs.at[s, 3], facs.at[s, 2], to(-1)
        place = 6 if kind == 7 else kind
        return pltpu.make_async_remote_copy(
            src_ref=src,
            dst_ref=dst,
            send_sem=wave_send.at[s, kind],
            recv_sem=wave_recv.at[s, place],
            device_id=dev,
            device_id_type=MESH,
        )

    def beam_at(s, k):
        beam = jnp.int32(0)
        for q in range(1, BEAMS):
            beam = jnp.where(offsets[s, q] == k, q, beam)
        return beam

    column = lax.broadcasted_iota(jnp.int32, (SIDE, SIDE), 1)

    def forward(s):
        rows = []
        for k in range(BEAMS):
            y = metas[k, s, 0]
            slab, shift = lane_start(metas[k, s, 1])
            turn = lax.rem(SIDE - shift, SIDE)
            beam = beam_at(s, k)
            z_re, z_im = [
                jnp.where(
                    column < SIDE - shift,
                    pltpu.roll(frame[c, slab, pl.ds(y, SIDE)], turn, 1),
                    pltpu.roll(frame[c, slab + 1, pl.ds(y, SIDE)], turn, 1),
                )
                for c in range(2)
            ]
            p_re, p_im = probe[beam, 0], probe[beam, 1]
            wave = jnp.concatenate([p_re * z_re - p_im * z_im, p_re * z_im + p_im * z_re], axis=1)
            psi[s, k * SIDE : (k + 1) * SIDE] = wave
            rows.append(wave)
        once = on_lanes(jnp.concatenate(rows, axis=0), high[0], low[0])
        once = jnp.concatenate(
            [
                jnp.concatenate([once[k * SIDE : (k + 1) * SIDE, q * SIDE : (q + 1) * SIDE] for k in range(BEAMS)], axis=1)
                for q in range(2)
            ],
            axis=0,
        )
        twice = on_rows(high[1], low[1], once)
        far[s] = twice
        for k in (2, 1, 3, 0):
            re = twice[:SIDE, k * SIDE : (k + 1) * SIDE]
            im = twice[SIDE:, k * SIDE : (k + 1) * SIDE]
            inten[s, k] = re * re + im * im
        for kind, wanted in ((0, by_third(s, 2) == 0), (1, by_third(s, 2) == 1), (2, by_third(s, 1) == 1), (3, by_third(s, 3) == 0)):

            @pl.when(wanted)
            def _(kind=kind):
                copy(s, kind).start()

    def join(s):
        for k, which, wanted in ((1, 0, by_third(s, 1) == 0), (3, 1, by_third(s, 3) == 1)):

            @pl.when(wanted)
            def _(k=k, which=which):
                copy(s, which).wait_recv()
                inten[s, k] = inten[s, k] + relay[s, which]
                copy(s, 2 + which).start()

    def settle(s):
        copy(s, 2).wait_recv()
        copy(s, 3).wait_recv()
        total = inten[s, 0] + gathered[s, 0] + gathered[s, 1]
        facs[s, 0] = measured[s] / jnp.sqrt(total + EPSILON)
        copy(s, 4).start()
        copy(s, 5).start()

    def hand_on(s):
        for k, which, wanted in ((1, 0, by_third(s, 1) == 0), (3, 1, by_third(s, 3) == 1)):

            @pl.when(wanted)
            def _(k=k, which=which):
                copy(s, 4 + which).wait_recv()
                copy(s, 6 + which).start()

    def place(s, channels):
        starts, picks = [], []
        for k in range(BEAMS):
            slab, shift = lane_start(metas[k, s, 1])
            starts.append(PAD - metas[k, s, 0])
            live = s < metas[k, 0, 2]
            for q, (channel, values) in enumerate(channels):
                turned = pltpu.roll(jnp.where(live, values[k], 0.0), shift, 1)
                at = 2 * (q * BEAMS + k)
                padded[at, PAD : PAD + SIDE] = jnp.where(column >= shift, turned, 0.0)
                padded[at + 1, PAD : PAD + SIDE] = jnp.where(column < shift, turned, 0.0)
            picks.append([jnp.where(slab == b, 0, jnp.where(slab + 1 == b, 1, 2)) for b in range(SLABS)])
        for q, (channel, values) in enumerate(channels):

            def add(row, carry, q=q, channel=channel):
                here = pl.ds(pl.multiple_of(row * HALF, HALF), HALF)
                for b in range(SLABS):
                    value = accum[channel, b, here]
                    for k in range(BEAMS):
                        at = jnp.where(picks[k][b] == 2, 4 * BEAMS, 2 * (q * BEAMS + k) + picks[k][b])
                        value = value + padded[at, pl.ds(starts[k] + row * HALF, HALF)]
                    accum[channel, b, here] = value
                return carry

            lax.fori_loop(0, TALL // HALF, add, 0)

    def weigh(s):
        values = []
        for k in range(BEAMS):
            beam = beam_at(s, k)
            p_re, p_im = probe[beam, 0], probe[beam, 1]
            values.append(p_re * p_re + p_im * p_im)
        place(s, [(2, values)])

    def back(s):
        for k, which, wanted in ((1, 0, by_third(s, 1) == 1), (3, 1, by_third(s, 3) == 0)):

            @pl.when(wanted)
            def _(which=which):
                copy(s, 4 + which).wait_recv()

        copy(s, 6).wait_recv()
        factor = jnp.concatenate([facs[s, k] for k in range(BEAMS)], axis=1)
        scaled = jnp.concatenate([far[s, :SIDE] * factor, far[s, SIDE:] * factor], axis=0)
        once = on_rows(high[0], low[0], scaled)
        once = jnp.concatenate(
            [
                jnp.concatenate([once[q * SIDE : (q + 1) * SIDE, k * SIDE : (k + 1) * SIDE] for q in range(2)], axis=1)
                for k in range(BEAMS)
            ],
            axis=0,
        )
        change = on_lanes(once, high[1], low[1]) - psi[s]
        re, im = [], []
        for k in range(BEAMS):
            beam = beam_at(s, k)
            p_re, p_im = probe[beam, 0], probe[beam, 1]
            c_re = change[k * SIDE : (k + 1) * SIDE, :SIDE]
            c_im = change[k * SIDE : (k + 1) * SIDE, SIDE:]
            re.append(p_re * c_re + p_im * c_im)
            im.append(p_re * c_im - p_im * c_re)
        place(s, [(0, re), (1, im)])

    ends = ((0, HALF, low_edge, up), (HALF, low_edge, HALF, None), (low_edge, TALL, 0, down))
    sides = ((0, left), (end, right))
    weight_plan = [
        (accum.at[2, 1:end, 0:HALF], weight_rows.at[1], {"row": up}),
        (accum.at[2, 1:end, low_edge:TALL], weight_rows.at[0], {"row": down}),
    ]
    rim_plan = [
        (accum.at[0:2, 1:end, 0:HALF], rows_in.at[1], {"row": up}),
        (accum.at[0:2, 1:end, low_edge:TALL], rows_in.at[0], {"row": down}),
    ]
    for side, (slab, to_col) in enumerate(sides):
        for first, stop, land, to_row in ends:
            dev = {"col": to_col} if to_row is None else {"row": to_row, "col": to_col}
            arrive = slice(land, land + stop - first)
            weight_plan.append((accum.at[2, slab, first:stop], weight_sides.at[side, arrive], dev))
            rim_plan.append((pack.at[side, first:stop], sides_in.at[side, arrive], dev))
    work = {"forward": forward, "weigh": weigh, "join": join, "settle": settle, "hand_on": hand_on, "back": back}

    def step(t, carry):
        for name, lag in STAGES:

            @pl.when(jnp.logical_and(t >= lag, t < SCANS + lag))
            def _(name=name, lag=lag):
                work[name](t - lag)

        @pl.when(t == WEIGHTS_AT)
        def _():
            exchange(weight_plan, 15)

        return carry

    lax.fori_loop(0, SCANS + STAGES[-1][1], step, 0)
    lane = lax.broadcasted_iota(jnp.int32, (TALL, SIDE), 1)
    pack[0] = jnp.where(lane >= HALF, accum[0, 0], pltpu.roll(accum[1, 0], HALF, 1))
    pack[1] = jnp.where(lane < HALF, accum[0, end], pltpu.roll(accum[1, end], HALF, 1))
    copies = exchange(rim_plan, 23)
    waits = [
        pltpu.make_async_remote_copy(
            src_ref=src, dst_ref=dst, send_sem=send.at[15 + q], recv_sem=recv.at[15 + q], device_id=dev, device_id_type=MESH
        )
        for q, (src, dst, dev) in enumerate(weight_plan)
    ]
    for one in waits:
        one.wait()

    def drain(s, carry):
        for kind in (2, 3, 4, 5):
            copy(s, kind).wait_send()
        for kind, wanted in (
            (0, by_third(s, 2) == 0),
            (1, by_third(s, 2) == 1),
            (6, by_third(s, 1) == 0),
            (7, by_third(s, 3) == 1),
        ):

            @pl.when(wanted)
            def _(kind=kind):
                copy(s, kind).wait_send()

        return carry

    lax.fori_loop(0, SCANS, drain, 0)
    for one in copies:
        one.wait()

    def kept(ok, value):
        return jnp.where(ok, value, 0.0)

    lane = lax.broadcasted_iota(jnp.int32, (TILE, SIDE), 1)

    def rim_column(ref, side):
        head = ref[side, HALF:SIDE] + kept(i > 0, ref[side, 0:HALF])
        tail = ref[side, TILE:low_edge] + kept(i < nr - 1, ref[side, low_edge:TALL])
        return jnp.concatenate([head, ref[side, SIDE:TILE], tail], axis=0)

    from_right, from_left = rim_column(sides_in, 0), rim_column(sides_in, 1)
    rights = (from_right, pltpu.roll(from_right, HALF, 1), rim_column(weight_sides, 0))
    lefts = (from_left, pltpu.roll(from_left, HALF, 1), rim_column(weight_sides, 1))
    for b in range(COLUMNS):
        sums = []
        for c in range(3):
            above = weight_rows[0, b] if c == 2 else rows_in[0, c, b]
            below = weight_rows[1, b] if c == 2 else rows_in[1, c, b]
            head = accum[c, b + 1, HALF:SIDE] + kept(i > 0, above)
            tail = accum[c, b + 1, TILE:low_edge] + kept(i < nr - 1, below)
            value = jnp.concatenate([head, accum[c, b + 1, SIDE:TILE], tail], axis=0)
            if b == 0:
                value = value + kept(jnp.logical_and(lane < HALF, j > 0), lefts[c])
            if b == COLUMNS - 1:
                value = value + kept(jnp.logical_and(lane >= HALF, j < nc - 1), rights[c])
            sums.append(value)
        part = slice(b * SIDE, (b + 1) * SIDE)
        for c in range(2):
            out[c, :, part] = obj[c, :, part] + sums[c] / (sums[2] + DAMPING)


def f32(*shape):
    return pltpu.VMEM(shape, jnp.float32)


def on_device(obj, probe, positions, counts, offsets, measured):
    nr, nc = lax.axis_size("row"), lax.axis_size("col")
    spots = positions[0, 0]
    count = jnp.broadcast_to(counts, (SCANS, 1))
    meta = jnp.pad(jnp.concatenate([spots, count], axis=1), ((0, 0), (0, SIDE - 3)))
    high, low = tables()
    dma = pltpu.SemaphoreType.DMA
    return pl.pallas_call(
        functools.partial(step_kernel, nr, nc),
        out_shape=jax.ShapeDtypeStruct((2, TILE, TILE), jnp.float32),
        in_specs=[ANY] * 5 + [VMEM, SMEM],
        out_specs=VMEM,
        scratch_shapes=[
            f32(2, TILE, TILE),
            f32(BEAMS, 2, SIDE, SIDE),
            f32(SCANS, SIDE, SIDE),
            pltpu.VMEM((2, 2 * SIDE, 2 * SIDE), jnp.bfloat16),
            pltpu.VMEM((2, 2 * SIDE, 2 * SIDE), jnp.bfloat16),
            pltpu.VMEM((BEAMS, SCANS, SIDE), jnp.int32),
            pltpu.SMEM((BEAMS, SCANS, SIDE), jnp.int32),
            f32(2, SLABS, TALL, SIDE),
            f32(2, TALL, SIDE),
            f32(SCANS, BEAMS * SIDE, 2 * SIDE),
            f32(SCANS, 2 * SIDE, BEAMS * SIDE),
            f32(SCANS, BEAMS, SIDE, SIDE),
            f32(SCANS, 2, SIDE, SIDE),
            f32(SCANS, 2, SIDE, SIDE),
            f32(SCANS, BEAMS, SIDE, SIDE),
            f32(4 * BEAMS + 1, 2 * PAD, SIDE),
            f32(3, SLABS, TALL, SIDE),
            f32(2, 2, COLUMNS, HALF, SIDE),
            f32(2, TALL, SIDE),
            f32(2, COLUMNS, HALF, SIDE),
            f32(2, TALL, SIDE),
            dma((6,)),
            dma((31,)),
            dma((31,)),
            dma((SCANS, 8)),
            dma((SCANS, 7)),
        ],
        compiler_params=pltpu.CompilerParams(collective_id=1, has_side_effects=True, vmem_limit_bytes=56 * 2**20),
        name="step",
    )(obj, probe, measured[0, 0], jnp.asarray(high), jnp.asarray(low), meta, offsets)


def solution(mesh):
    return jax.shard_map(
        on_device,
        mesh=mesh,
        in_specs=(
            P(None, "row", "col"),
            P(),
            P("row", "col", None, None),
            P("row", "col"),
            P(),
            P("row", "col", None, None, None),
        ),
        out_specs=P(None, "row", "col"),
        check_vma=False,
    )
```

time: 118 us -> 102 us (0.86)
  Pallas kernels: 107 us -> 95.1 us
  local copies, waits for them, and re-layouts: 7.78 us -> 4.46 us
    pallas_call x4 -> x1, Pallas kernels: 107 us -> 95.1 us  [on_device(): pl.pallas_call(functools.partial(step_kernel, nr, nc), out_shape=jax.Shap...]
    unnamed x14 -> x2, local copies, waits for them, and re-layouts: 7.03 us -> 3.71 us
where the time goes in v2:
time: 102 us; the launch traced here: 101 us
  Pallas kernels  95.1 us (93%)
  local copies, waits for them, and re-layouts  4.46 us (4%)
    pallas_call x1, Pallas kernels, on_device(): pl.pallas_call(functools.partial(step_kernel, nr, nc), out_shape=jax.Shap...  95.1 us
    unnamed x2, local copies, waits for them, and re-layouts  3.71 us

profile of v2, /device:TPU:13, one launch (start us, length us, event | category | flops | bytes accessed | tf_op | source)
XLA Modules:
  0.0 100.9 jit_solution(6573642245936145121)
XLA Ops:
  0.7 0.8 copy.9
  1.4 0.6 pad_select_fusion.meta
  2.0 1.3 %copy.10.offsets = s32[8,4]{1,0:T(8,128)} copy(s32[8,4]{0,1:T(4,128)} %param.12) | data formatting | bytes 256 | tf_op args[4]
  3.4 95.1 %step.1 = f32[2,384,384]{2,1,0:T(8,128)} custom-call(f32[2,384,384]{2,1,0:T(8,128)} %obj_hbm.1, f32[4,2,128,128]{3,2,1,0:T(8,128)} %probe_hbm.1, f32[8,128,128]{2,1,0:T(8,128)} %bitcast.4, bf16[2,256,256]{2,1,0:T(8,128)(2,1)} %constant.6.clone.high_hbm, bf16[2,256,256]{2,1,0:T(8,128)(2,1)} %constant.7.clone.low_hbm, s32[8,128]{1,0:T(8,128)} %pad_select_fusion.meta, ...), custom_call_target="tpu_custom_call" | custom-call | tf_op jit(solution)/shard_map/step/pallas_call | solution.py:456
  98.5 2.4 %copy.13 = f32[2,384,384]{2,1,0:T(8,128)} copy(f32[2,384,384]{2,1,0:T(8,128)} %step.1) | data formatting | bytes 2359296

commit v3 on v2

--- a/solution.py
+++ b/solution.py
@@ -22,10 +22,9 @@
 MESH = pl.DeviceIdType.MESH
 VMEM = pl.BlockSpec(memory_space=pltpu.VMEM)
 SMEM = pl.BlockSpec(memory_space=pltpu.SMEM)
-ANY = pl.BlockSpec(memory_space=pl.ANY)
+HBM = pl.BlockSpec(memory_space=pltpu.HBM)
 PAD = 512
-STAGES = (("forward", 0), ("weigh", 2), ("join", 2), ("settle", 4), ("hand_on", 6), ("back", 8))
-WEIGHTS_AT = 12
+STAGES = (("forward", 0), ("join", 1), ("settle", 2), ("hand_on", 3), ("back", 4))
 
 
 def tables():
@@ -65,8 +64,8 @@
     return slab, at - slab * SIDE
 
 
-def ROUTE(z, s):
-    return lax.rem(s, 2)
+def by_fourth(z, s):
+    return jnp.where(z == 1, 0, jnp.where(z == 2, 1, lax.rem(s, 2)))
 
 
 def neighbours(i, j, nr, nc):
@@ -76,9 +75,9 @@
 
 
 def step_kernel(
-    nr, nc, obj_hbm, probe_hbm, measured_hbm, high_hbm, low_hbm, meta, offsets, out,
-    obj, probe, measured, high, low, metas_in, metas, frame, pack, psi, far, inten, relay, gathered, facs,
-    padded, accum, rows_in, sides_in, weight_rows, weight_sides, local, send, recv, wave_send, wave_recv,
+    nr, nc, obj_hbm, probe_hbm, measured_hbm, high_hbm, low_hbm, positions, counts, offsets, out,
+    obj, probe, measured, high, low, meta, metas_in, metas, frame, pack, psi, far, inten, relay, gathered, facs,
+    padded, accum, rows_in, sides_in, weight_pack, weight_rows, weight_sides, local, send, recv, wave_send, wave_recv,
 ):
     i, j = lax.axis_index("row"), lax.axis_index("col")
     up, down, left, right = neighbours(i, j, nr, nc)
@@ -97,19 +96,13 @@
     ]
     for fetch in fetches:
         fetch.start()
-    metas_in[0] = meta[...]
-
-    def clear(q, carry):
-        padded[q] = jnp.zeros((2 * PAD, SIDE), jnp.float32)
-        return carry
-
-    lax.fori_loop(0, 4 * BEAMS + 1, clear, 0)
-
-    def clear_sum(q, carry):
-        accum[lax.div(q, SLABS), lax.rem(q, SLABS)] = jnp.zeros((TALL, SIDE), jnp.float32)
-        return carry
-
-    lax.fori_loop(0, 3 * SLABS, clear_sum, 0)
+    row, item = [lax.broadcasted_iota(jnp.int32, (SCANS, SIDE), d) for d in range(2)]
+    packed = jnp.where(item == 2, counts[0, 0], 0)
+    for s in range(SCANS):
+        for c in range(2):
+            packed = jnp.where(jnp.logical_and(row == s, item == c), positions[c, s], packed)
+    meta[...] = packed
+    metas_in[0] = packed
     fetches[0].wait()
     lane = lax.broadcasted_iota(jnp.int32, (TILE, SIDE), 1)
     low_edge, top, end, last = HALF + TILE, TILE - HALF, SLABS - 1, TILE - SIDE
@@ -150,15 +143,94 @@
     copies = exchange(plan, 0)
     for b in range(COLUMNS):
         frame[:, b + 1, HALF:low_edge] = obj[:, :, b * SIDE : (b + 1) * SIDE]
+
+    def clear(q, carry):
+        padded[q] = jnp.zeros((2 * PAD, SIDE), jnp.float32)
+        return carry
+
+    lax.fori_loop(0, 4 * BEAMS + 1, clear, 0)
+
+    def clear_sum(q, carry):
+        accum[lax.div(q, SLABS), lax.rem(q, SLABS)] = jnp.zeros((TALL, SIDE), jnp.float32)
+        return carry
+
+    lax.fori_loop(0, 3 * SLABS, clear_sum, 0)
     for fetch in fetches[1:]:
         fetch.wait()
     for one in copies[:3]:
         one.wait()
     settled = pltpu.make_async_copy(metas_in, metas, local.at[5])
     settled.start()
+    settled.wait()
+    column = lax.broadcasted_iota(jnp.int32, (SIDE, SIDE), 1)
+
+    def beam_at(s, k):
+        beam = jnp.int32(0)
+        for q in range(1, BEAMS):
+            beam = jnp.where(offsets[q, s] == k, q, beam)
+        return beam
+
+    def place(s, channels):
+        starts, picks = [], []
+        for k in range(BEAMS):
+            slab, shift = lane_start(metas[k, s, 1])
+            starts.append(PAD - metas[k, s, 0])
+            live = s < metas[k, 0, 2]
+            for q, (channel, values) in enumerate(channels):
+                turned = pltpu.roll(jnp.where(live, values[k], 0.0), shift, 1)
+                at = 2 * (q * BEAMS + k)
+                padded[at, PAD : PAD + SIDE] = jnp.where(column >= shift, turned, 0.0)
+                padded[at + 1, PAD : PAD + SIDE] = jnp.where(column < shift, turned, 0.0)
+            picks.append([jnp.where(slab == b, 0, jnp.where(slab + 1 == b, 1, 2)) for b in range(SLABS)])
+        for q, (channel, values) in enumerate(channels):
+
+            def add(row, carry, q=q, channel=channel):
+                here = pl.ds(pl.multiple_of(row * HALF, HALF), HALF)
+                for b in range(SLABS):
+                    value = accum[channel, b, here]
+                    for k in range(BEAMS):
+                        at = jnp.where(picks[k][b] == 2, 4 * BEAMS, 2 * (q * BEAMS + k) + picks[k][b])
+                        value = value + padded[at, pl.ds(starts[k] + row * HALF, HALF)]
+                    accum[channel, b, here] = value
+                return carry
+
+            lax.fori_loop(0, TALL // HALF, add, 0)
+
+    def weigh(s):
+        values = []
+        for k in range(BEAMS):
+            beam = beam_at(s, k)
+            p_re, p_im = probe[beam, 0], probe[beam, 1]
+            values.append(p_re * p_re + p_im * p_im)
+        place(s, [(2, values)])
+
+    def weigh_one(s, carry):
+        weigh(s)
+        return carry
+
+    lax.fori_loop(0, SCANS, weigh_one, 0)
+    half_lane = lax.broadcasted_iota(jnp.int32, (HALF, SIDE), 1)
+    folds = [(q * HALF, (q + 3) * HALF) for q in range(1, 4)] + [(0, low_edge)]
+    for side, slab in ((0, 0), (1, end)):
+        for q, (first, second) in enumerate(folds):
+            straight = accum[2, slab, first : first + HALF]
+            folded = pltpu.roll(accum[2, slab, second : second + HALF], HALF, 1)
+            keep = half_lane >= HALF if side == 0 else half_lane < HALF
+            weight_pack[side, q * HALF : (q + 1) * HALF] = jnp.where(keep, straight, folded)
+    mid, fold_rows = slice(0, 3 * HALF), slice(3 * HALF, 4 * HALF)
+    weight_plan = [
+        (accum.at[2, 1:end, 0:HALF], weight_rows.at[1], {"row": up}),
+        (accum.at[2, 1:end, low_edge:TALL], weight_rows.at[0], {"row": down}),
+    ]
+    for side, to_col in ((0, left), (1, right)):
+        weight_plan += [
+            (weight_pack.at[side, mid], weight_sides.at[side, mid], {"col": to_col}),
+            (weight_pack.at[side, fold_rows], weight_sides.at[side, 4 * HALF : 5 * HALF], {"row": up, "col": to_col}),
+            (weight_pack.at[side, fold_rows], weight_sides.at[side, fold_rows], {"row": down, "col": to_col}),
+        ]
+    weight_copies = exchange(weight_plan, 15)
     for one in copies[3:]:
         one.wait()
-    settled.wait()
     for slab in (0, end):
         frame[1, slab] = pltpu.roll(frame[0, slab], HALF, 1)
 
@@ -182,7 +254,7 @@
         return {"row": lax.rem(i + by + nr, nr)}
 
     def by_third(s, k):
-        return ROUTE(lax.rem(i + nr - k, 4), s)
+        return by_fourth(lax.rem(i + nr - k, 4), s)
 
     def copy(s, kind):
         if kind == 0:
@@ -210,14 +282,6 @@
             device_id=dev,
             device_id_type=MESH,
         )
-
-    def beam_at(s, k):
-        beam = jnp.int32(0)
-        for q in range(1, BEAMS):
-            beam = jnp.where(offsets[s, q] == k, q, beam)
-        return beam
-
-    column = lax.broadcasted_iota(jnp.int32, (SIDE, SIDE), 1)
 
     def forward(s):
         rows = []
@@ -283,40 +347,6 @@
                 copy(s, 4 + which).wait_recv()
                 copy(s, 6 + which).start()
 
-    def place(s, channels):
-        starts, picks = [], []
-        for k in range(BEAMS):
-            slab, shift = lane_start(metas[k, s, 1])
-            starts.append(PAD - metas[k, s, 0])
-            live = s < metas[k, 0, 2]
-            for q, (channel, values) in enumerate(channels):
-                turned = pltpu.roll(jnp.where(live, values[k], 0.0), shift, 1)
-                at = 2 * (q * BEAMS + k)
-                padded[at, PAD : PAD + SIDE] = jnp.where(column >= shift, turned, 0.0)
-                padded[at + 1, PAD : PAD + SIDE] = jnp.where(column < shift, turned, 0.0)
-            picks.append([jnp.where(slab == b, 0, jnp.where(slab + 1 == b, 1, 2)) for b in range(SLABS)])
-        for q, (channel, values) in enumerate(channels):
-
-            def add(row, carry, q=q, channel=channel):
-                here = pl.ds(pl.multiple_of(row * HALF, HALF), HALF)
-                for b in range(SLABS):
-                    value = accum[channel, b, here]
-                    for k in range(BEAMS):
-                        at = jnp.where(picks[k][b] == 2, 4 * BEAMS, 2 * (q * BEAMS + k) + picks[k][b])
-                        value = value + padded[at, pl.ds(starts[k] + row * HALF, HALF)]
-                    accum[channel, b, here] = value
-                return carry
-
-            lax.fori_loop(0, TALL // HALF, add, 0)
-
-    def weigh(s):
-        values = []
-        for k in range(BEAMS):
-            beam = beam_at(s, k)
-            p_re, p_im = probe[beam, 0], probe[beam, 1]
-            values.append(p_re * p_re + p_im * p_im)
-        place(s, [(2, values)])
-
     def back(s):
         for k, which, wanted in ((1, 0, by_third(s, 1) == 1), (3, 1, by_third(s, 3) == 0)):
 
@@ -348,10 +378,6 @@
 
     ends = ((0, HALF, low_edge, up), (HALF, low_edge, HALF, None), (low_edge, TALL, 0, down))
     sides = ((0, left), (end, right))
-    weight_plan = [
-        (accum.at[2, 1:end, 0:HALF], weight_rows.at[1], {"row": up}),
-        (accum.at[2, 1:end, low_edge:TALL], weight_rows.at[0], {"row": down}),
-    ]
     rim_plan = [
         (accum.at[0:2, 1:end, 0:HALF], rows_in.at[1], {"row": up}),
         (accum.at[0:2, 1:end, low_edge:TALL], rows_in.at[0], {"row": down}),
@@ -360,9 +386,8 @@
         for first, stop, land, to_row in ends:
             dev = {"col": to_col} if to_row is None else {"row": to_row, "col": to_col}
             arrive = slice(land, land + stop - first)
-            weight_plan.append((accum.at[2, slab, first:stop], weight_sides.at[side, arrive], dev))
             rim_plan.append((pack.at[side, first:stop], sides_in.at[side, arrive], dev))
-    work = {"forward": forward, "weigh": weigh, "join": join, "settle": settle, "hand_on": hand_on, "back": back}
+    work = {"forward": forward, "join": join, "settle": settle, "hand_on": hand_on, "back": back}
 
     def step(t, carry):
         for name, lag in STAGES:
@@ -370,10 +395,6 @@
             @pl.when(jnp.logical_and(t >= lag, t < SCANS + lag))
             def _(name=name, lag=lag):
                 work[name](t - lag)
-
-        @pl.when(t == WEIGHTS_AT)
-        def _():
-            exchange(weight_plan, 15)
 
         return carry
 
@@ -382,13 +403,7 @@
     pack[0] = jnp.where(lane >= HALF, accum[0, 0], pltpu.roll(accum[1, 0], HALF, 1))
     pack[1] = jnp.where(lane < HALF, accum[0, end], pltpu.roll(accum[1, end], HALF, 1))
     copies = exchange(rim_plan, 23)
-    waits = [
-        pltpu.make_async_remote_copy(
-            src_ref=src, dst_ref=dst, send_sem=send.at[15 + q], recv_sem=recv.at[15 + q], device_id=dev, device_id_type=MESH
-        )
-        for q, (src, dst, dev) in enumerate(weight_plan)
-    ]
-    for one in waits:
+    for one in weight_copies:
         one.wait()
 
     def drain(s, carry):
@@ -422,8 +437,15 @@
         return jnp.concatenate([head, ref[side, SIDE:TILE], tail], axis=0)
 
     from_right, from_left = rim_column(sides_in, 0), rim_column(sides_in, 1)
-    rights = (from_right, pltpu.roll(from_right, HALF, 1), rim_column(weight_sides, 0))
-    lefts = (from_left, pltpu.roll(from_left, HALF, 1), rim_column(weight_sides, 1))
+
+    def weight_column(side):
+        turned = [pltpu.roll(weight_sides[side, q * HALF : (q + 1) * HALF], HALF, 1) for q in range(4)]
+        head = weight_sides[side, 0:HALF] + kept(i > 0, turned[3])
+        tail = turned[2] + kept(i < nr - 1, weight_sides[side, 4 * HALF : 5 * HALF])
+        return jnp.concatenate([head, weight_sides[side, HALF : 3 * HALF], turned[0], turned[1], tail], axis=0)
+
+    rights = (from_right, pltpu.roll(from_right, HALF, 1), weight_column(0))
+    lefts = (from_left, pltpu.roll(from_left, HALF, 1), weight_column(1))
     for b in range(COLUMNS):
         sums = []
         for c in range(3):
@@ -448,15 +470,12 @@
 
 def on_device(obj, probe, positions, counts, offsets, measured):
     nr, nc = lax.axis_size("row"), lax.axis_size("col")
-    spots = positions[0, 0]
-    count = jnp.broadcast_to(counts, (SCANS, 1))
-    meta = jnp.pad(jnp.concatenate([spots, count], axis=1), ((0, 0), (0, SIDE - 3)))
     high, low = tables()
     dma = pltpu.SemaphoreType.DMA
     return pl.pallas_call(
         functools.partial(step_kernel, nr, nc),
-        out_shape=jax.ShapeDtypeStruct((2, TILE, TILE), jnp.float32),
-        in_specs=[ANY] * 5 + [VMEM, SMEM],
+        out_shape=pltpu.VMEM((2, TILE, TILE), jnp.float32),
+        in_specs=[HBM] * 5 + [SMEM] * 3,
         out_specs=VMEM,
         scratch_shapes=[
             f32(2, TILE, TILE),
@@ -464,6 +483,7 @@
             f32(SCANS, SIDE, SIDE),
             pltpu.VMEM((2, 2 * SIDE, 2 * SIDE), jnp.bfloat16),
             pltpu.VMEM((2, 2 * SIDE, 2 * SIDE), jnp.bfloat16),
+            pltpu.VMEM((SCANS, SIDE), jnp.int32),
             pltpu.VMEM((BEAMS, SCANS, SIDE), jnp.int32),
             pltpu.SMEM((BEAMS, SCANS, SIDE), jnp.int32),
             f32(2, SLABS, TALL, SIDE),
@@ -478,17 +498,18 @@
             f32(3, SLABS, TALL, SIDE),
             f32(2, 2, COLUMNS, HALF, SIDE),
             f32(2, TALL, SIDE),
+            f32(2, 4 * HALF, SIDE),
             f32(2, COLUMNS, HALF, SIDE),
-            f32(2, TALL, SIDE),
+            f32(2, 5 * HALF, SIDE),
             dma((6,)),
             dma((31,)),
             dma((31,)),
             dma((SCANS, 8)),
             dma((SCANS, 7)),
         ],
-        compiler_params=pltpu.CompilerParams(collective_id=1, has_side_effects=True, vmem_limit_bytes=56 * 2**20),
+        compiler_params=pltpu.CompilerParams(collective_id=1, has_side_effects=True, vmem_limit_bytes=54 * 2**20),
         name="step",
-    )(obj, probe, measured[0, 0], jnp.asarray(high), jnp.asarray(low), meta, offsets)
+    )(obj, probe, measured[0, 0], jnp.asarray(high), jnp.asarray(low), positions[0, 0].T, counts, offsets.T)
 
 
 def solution(mesh):

time: 102 us -> 89.7 us (0.88)
  Pallas kernels: 95.1 us -> 87.4 us
  local copies, waits for them, and re-layouts: 4.46 us -> 1.02 us
    pallas_call x1, Pallas kernels: 95.1 us -> 87.4 us  [on_device(): pl.pallas_call(functools.partial(step_kernel, nr, nc), out_shape=pltpu.VM...]
    unnamed x2 -> x1, local copies, waits for them, and re-layouts: 3.71 us -> 1.02 us
where the time goes in v3:
time: 89.7 us; the launch traced here: 89 us
  Pallas kernels  87.4 us (97%)
  local copies, waits for them, and re-layouts  1.02 us (1%)
    pallas_call x1, Pallas kernels, on_device(): pl.pallas_call(functools.partial(step_kernel, nr, nc), out_shape=pltpu.VM...  87.4 us

profile of v3, /device:TPU:13, one launch (start us, length us, event | category | flops | bytes accessed | tf_op | source)
XLA Modules:
  0.0 89.0 jit_solution(16490500649248396239)
XLA Ops:
  0.7 87.4 %step.1 = f32[2,384,384]{2,1,0:T(8,128)S(1)} custom-call(f32[2,384,384]{2,1,0:T(8,128)} %obj_hbm.1, f32[4,2,128,128]{3,2,1,0:T(8,128)} %probe_hbm.1, f32[8,128,128]{2,1,0:T(8,128)} %bitcast.5, bf16[2,256,256]{2,1,0:T(8,128)(2,1)} %constant.4.clone.high_hbm, bf16[2,256,256]{2,1,0:T(8,128)(2,1)} %constant.5.clone.low_hbm, s32[2,8]{1,0:T(2,128)} %bitcast.7, ...), custom_call_target="tpu_custom_call" | custom-call | tf_op jit(solution)/shard_map/step/pallas_call | solution.py:475
  88.0 1.0 %copy.10 = f32[2,384,384]{2,1,0:T(8,128)} copy(f32[2,384,384]{2,1,0:T(8,128)S(1)} %step.1) | data formatting | bytes 2359296

commit v4 on v3

--- a/solution.py
+++ b/solution.py
@@ -65,7 +65,7 @@
 
 
 def by_fourth(z, s):
-    return jnp.where(z == 1, 0, jnp.where(z == 2, 1, lax.rem(s, 2)))
+    return jnp.where(z == 1, 0, jnp.where(z >= 2, 1, lax.rem(s, 2)))
 
 
 def neighbours(i, j, nr, nc):

time: 89.7 us -> 88.5 us (0.987)
  Pallas kernels: 87.4 us -> 86.2 us
    pallas_call x1, Pallas kernels: 87.4 us -> 86.2 us  [on_device(): pl.pallas_call(functools.partial(step_kernel, nr, nc), out_shape=pltpu.VM...]
where the time goes in v4:
time: 88.5 us; the launch traced here: 87.9 us
  Pallas kernels  86.2 us (97%)
  local copies, waits for them, and re-layouts  1.02 us (1%)
    pallas_call x1, Pallas kernels, on_device(): pl.pallas_call(functools.partial(step_kernel, nr, nc), out_shape=pltpu.VM...  86.2 us

profile of v4, /device:TPU:13, one launch (start us, length us, event | category | flops | bytes accessed | tf_op | source)
XLA Modules:
  0.0 87.9 jit_solution(15433975316659433623)
XLA Ops:
  0.7 86.2 %step.1 = f32[2,384,384]{2,1,0:T(8,128)S(1)} custom-call(f32[2,384,384]{2,1,0:T(8,128)} %obj_hbm.1, f32[4,2,128,128]{3,2,1,0:T(8,128)} %probe_hbm.1, f32[8,128,128]{2,1,0:T(8,128)} %bitcast.5, bf16[2,256,256]{2,1,0:T(8,128)(2,1)} %constant.4.clone.high_hbm, bf16[2,256,256]{2,1,0:T(8,128)(2,1)} %constant.5.clone.low_hbm, s32[2,8]{1,0:T(2,128)} %bitcast.7, ...), custom_call_target="tpu_custom_call" | custom-call | tf_op jit(solution)/shard_map/step/pallas_call | solution.py:475
  86.9 1.0 %copy.10 = f32[2,384,384]{2,1,0:T(8,128)} copy(f32[2,384,384]{2,1,0:T(8,128)S(1)} %step.1) | data formatting | bytes 2359296
